TPU v7x, 32 devices: a whole 2x2x4 slice. The times are simulated.
32 devices in a mesh: ctx: 8 (over z, y), head: 4 (over x, core).
Axes of the slice: x: 2, y: 2, z: 4, core: 2. Of those that a mesh axis runs over, the one named last changes fastest.
Arguments:
- query_input: bfloat16 [4096, 4096], P(('ctx', 'head')), may hold values from -6 to 6
- key_input: bfloat16 [4096, 4096], P(('ctx', 'head')), may hold values from -6 to 6
- value_input: bfloat16 [4096, 4096], P(('ctx', 'head')), may hold values from -6 to 6
- cotangent: bfloat16 [4096, 4096], P(('ctx', 'head')), may hold values from -6 to 6
- level_codes: int32 [32, 13, 4096], P('head', None, 'ctx'), may hold values from 0 to 15
Outputs:
- attended: bfloat16 [4096, 4096], P(('ctx', 'head'))
- grad_queries: bfloat16 [4096, 4096], P(('ctx', 'head'))
- grad_keys: bfloat16 [4096, 4096], P(('ctx', 'head'))
- grad_values: bfloat16 [4096, 4096], P(('ctx', 'head'))
All inputs are finite; a program needn't handle non-finite values.
Results may differ from a plain program's by a relative error of at most 0.0074.
Values may be sent and summed in bfloat16 or wider, within the bound.
No kernel may reach another device: no remote copies, remote signals or barrier semaphores. Data moves between devices by JAX's collectives and lax.ppermute only.
A program may use at most 128 MiB of HBM per device.

v0:
```python
import jax
import jax.numpy as jnp
from jax import lax
from jax.sharding import PartitionSpec as P


def swapped(block, axis, stride):
    count = lax.axis_size(axis)
    route = []
    for low in range(count):
        high = low | 1 << stride
        if high != low and high < count:
            route += [(low, high), (high, low)]
    return lax.ppermute(block, axis, route)


def level_gain(level):
    if level == 0:
        return 1.0
    return 2.0 ** (-(level - 1) / 2.0)


def member_of(owner_block, member_block, bit_index):
    bit_span = 2**bit_index
    owner_set = owner_block // bit_span % 2 == 1
    member_clear = member_block // bit_span % 2 == 0
    same_parent = owner_block // (2 * bit_span) == member_block // (2 * bit_span)
    return jnp.where(owner_set & member_clear & same_parent, 1.0, 0.0).astype(jnp.float32)


def on_device(query_input, key_input, value_input, cotangent, level_codes):
    query_rows, key_rows, value_rows, cot_rows = (
        lax.all_to_all(query_input, "head", split_axis=1, concat_axis=0, tiled=True),
        lax.all_to_all(key_input, "head", split_axis=1, concat_axis=0, tiled=True),
        lax.all_to_all(value_input, "head", split_axis=1, concat_axis=0, tiled=True),
        lax.all_to_all(cotangent, "head", split_axis=1, concat_axis=0, tiled=True),
    )
    head_count = level_codes.shape[0]
    total_levels = level_codes.shape[1]
    length = query_rows.shape[0]
    head_dim = query_rows.shape[1] // head_count
    tok_bits = length.bit_length() - 1
    ctx_bits = total_levels - tok_bits - 1
    score_scale = head_dim ** (-0.5)
    head_shape = (length, head_count, head_dim)
    query_heads = query_rows.reshape(head_shape)
    key_heads = key_rows.reshape(head_shape)
    value_heads = value_rows.reshape(head_shape)
    cot_heads = cot_rows.reshape(head_shape)
    code_weights = level_codes.astype(jnp.float32) / 8.0
    my_block = lax.axis_index("ctx")
    cross_scale = jnp.stack(
        [
            code_weights[:, tok_bits + 1 + bit_index, :]
            * (score_scale * level_gain(tok_bits + 1 + bit_index))
            * (my_block // 2**bit_index % 2).astype(jnp.float32)
            for bit_index in range(ctx_bits)
        ]
    )
    row_scale = jnp.transpose(cross_scale, (0, 2, 1))
    block_state = jnp.einsum(
        "phd,phe->hde", key_heads, value_heads, preferred_element_type=jnp.float32
    )
    scaled_cot = (row_scale[..., None] * cot_heads[None]).astype(jnp.bfloat16)
    grad_state = jnp.einsum(
        "phd,bphe->bhde", query_heads, scaled_cot, preferred_element_type=jnp.float32
    )
    running = block_state
    bucket_list = []
    for bit_index in range(ctx_bits):
        partner = swapped(running, "ctx", bit_index)
        bit_set = (my_block // 2**bit_index % 2).astype(jnp.float32)
        bucket_list.append(bit_set * partner)
        running = running + partner
    bucket_sums = jnp.stack(bucket_list)
    bucket = bucket_sums.astype(jnp.bfloat16)
    term_rows = head_count * head_dim
    targets = jnp.arange(term_rows * lax.axis_size("ctx") // term_rows, dtype=jnp.int32)
    chosen = jnp.stack(
        [member_of(my_block, targets, bit_index) for bit_index in range(ctx_bits)], axis=1
    )
    spread = jnp.einsum("tb,bhde->thde", chosen, grad_state, precision=lax.Precision.HIGHEST)
    pulled = lax.psum_scatter(
        spread.reshape(term_rows * lax.axis_size("ctx"), head_dim),
        "ctx",
        scatter_dimension=0,
        tiled=True,
    ).reshape(head_count, head_dim, head_dim)
    pulled_half = pulled.astype(jnp.bfloat16)
    block_rows = min(512, length)
    steps_count = length // block_rows
    places = jnp.arange(length, dtype=jnp.int32)

    def row_step(carried_grads, block_index):
        key_grad, value_grad = carried_grads
        first_row = block_index * block_rows
        rows_at = first_row + jnp.arange(block_rows, dtype=jnp.int32)
        levels = jnp.zeros((block_rows, length), jnp.int32)
        for bit_index in range(tok_bits):
            levels = levels + (
                rows_at[:, None] // 2**bit_index != places[None, :] // 2**bit_index
            ).astype(jnp.int32)
        weight = jnp.zeros((head_count, block_rows, length), jnp.float32)
        for level_index in range(tok_bits + 1):
            weight = jnp.where(
                (levels == level_index)[None],
                code_weights[:, level_index, :, None] * level_gain(level_index),
                weight,
            )
        weight = jnp.where((places[None, :] <= rows_at[:, None])[None], weight, 0.0)
        scores = jnp.einsum(
            "phd,shd->hps", query_heads, key_heads, preferred_element_type=jnp.float32
        )
        attention = (score_scale * weight * scores).astype(jnp.bfloat16)
        local_out = jnp.einsum(
            "hps,she->phe", attention, value_heads, preferred_element_type=jnp.float32
        )
        dots = jnp.einsum(
            "phe,she->hps", cot_heads, value_heads, preferred_element_type=jnp.float32
        )
        score_grads = (score_scale * weight * dots).astype(jnp.bfloat16)
        local_qgrad = jnp.einsum(
            "hps,shd->phd", score_grads, key_heads, preferred_element_type=jnp.float32
        )
        key_grad = key_grad + jnp.einsum(
            "hps,phd->shd", score_grads, query_heads, preferred_element_type=jnp.float32
        )
        value_grad = value_grad + jnp.einsum(
            "hps,phe->she", attention, cot_heads, preferred_element_type=jnp.float32
        )
        return ((key_grad, value_grad), (local_out, local_qgrad))

    zero_grads = jnp.zeros(head_shape, jnp.float32)
    (key_local, value_local), (local_out, local_qgrad) = lax.scan(
        row_step, (zero_grads, zero_grads), jnp.arange(steps_count, dtype=jnp.int32)
    )
    local_out = local_out.reshape(head_shape)
    local_qgrad = local_qgrad.reshape(head_shape)
    cross_out = jnp.sum(
        row_scale[..., None]
        * jnp.einsum("phd,bhde->bphe", query_heads, bucket, preferred_element_type=jnp.float32),
        axis=0,
    )
    cross_qgrad = jnp.sum(
        row_scale[..., None]
        * jnp.einsum("phe,bhde->bphd", cot_heads, bucket, preferred_element_type=jnp.float32),
        axis=0,
    )
    flat_shape = (length, head_count * head_dim)
    attended = (local_out + cross_out).astype(jnp.bfloat16).reshape(flat_shape)
    grad_query = (local_qgrad + cross_qgrad).astype(jnp.bfloat16).reshape(flat_shape)
    grad_key = (
        (
            key_local
            + jnp.einsum(
                "phe,hde->phd", value_heads, pulled_half, preferred_element_type=jnp.float32
            )
        )
        .astype(jnp.bfloat16)
        .reshape(flat_shape)
    )
    grad_value = (
        (
            value_local
            + jnp.einsum("phd,hde->phe", key_heads, pulled_half, preferred_element_type=jnp.float32)
        )
        .astype(jnp.bfloat16)
        .reshape(flat_shape)
    )
    return (
        lax.all_to_all(attended, "head", split_axis=0, concat_axis=1, tiled=True),
        lax.all_to_all(grad_query, "head", split_axis=0, concat_axis=1, tiled=True),
        lax.all_to_all(grad_key, "head", split_axis=0, concat_axis=1, tiled=True),
        lax.all_to_all(grad_value, "head", split_axis=0, concat_axis=1, tiled=True),
    )


def solution(mesh):
    return jax.shard_map(
        on_device,
        mesh=mesh,
        in_specs=(
            P(("ctx", "head"), None),
            P(("ctx", "head"), None),
            P(("ctx", "head"), None),
            P(("ctx", "head"), None),
            P("head", None, "ctx"),
        ),
        out_specs=(
            P(("ctx", "head"), None),
            P(("ctx", "head"), None),
            P(("ctx", "head"), None),
            P(("ctx", "head"), None),
        ),
        check_vma=False,
    )
```

profile of v0, /device:TPU:0, one launch (start us, length us, event | category | flops | bytes accessed | tf_op | source)
XLA Modules:
  0.0 264.9 jit_solution(6928649475833172917)
XLA Ops:
  7.2 2.4 copy.203
  9.5 4.4 %all-to-all-start = ((bf16[128,4,1024]{2,0,1:T(8,128)(2,1)}), bf16[128,4,1024]{2,0,1:T(8,128)(2,1)S(1)}, u32[]{:S(2)}, u32[]{:S(2)}) async-start(bf16[128,4,1024]{2,0,1:T(8,128)(2,1)} %bitcast.123), calls=%async_computation | async-start | bytes 2097152 | tf_op jit(solution)/shard_map/all_to_all | solution.py:33
  15.0 13.4 %all-to-all-done = bf16[128,4,1024]{2,0,1:T(8,128)(2,1)S(1)} async-done(((bf16[128,4,1024]{2,0,1:T(8,128)(2,1)}), bf16[128,4,1024]{2,0,1:T(8,128)(2,1)S(1)}, u32[]{:S(2)}, u32[]{:S(2)}) %all-to-all-start) | async-done | bytes 1048608 | tf_op jit(solution)/shard_map/all_to_all | solution.py:33
  28.3 3.5 %all-to-all-start.4 = ((bf16[128,4,1024]{2,0,1:T(8,128)(2,1)}), bf16[128,4,1024]{2,0,1:T(8,128)(2,1)S(1)}, u32[]{:S(2)}, u32[]{:S(2)}) async-start(bf16[128,4,1024]{2,0,1:T(8,128)(2,1)} %bitcast.120), calls=%async_computation.4 | async-start | bytes 2097152 | tf_op jit(solution)/shard_map/all_to_all | solution.py:36
  36.0 10.3 %all-to-all-done.4 = bf16[128,4,1024]{2,0,1:T(8,128)(2,1)S(1)} async-done(((bf16[128,4,1024]{2,0,1:T(8,128)(2,1)}), bf16[128,4,1024]{2,0,1:T(8,128)(2,1)S(1)}, u32[]{:S(2)}, u32[]{:S(2)}) %all-to-all-start.4) | async-done | bytes 1048608 | tf_op jit(solution)/shard_map/all_to_all | solution.py:36
  46.3 4.3 %all-to-all-start.1 = ((bf16[128,4,1024]{2,0,1:T(8,128)(2,1)}), bf16[128,4,1024]{2,0,1:T(8,128)(2,1)}, u32[]{:S(2)}, u32[]{:S(2)}) async-start(bf16[128,4,1024]{2,0,1:T(8,128)(2,1)} %bitcast.122), calls=%async_computation.1 | async-start | bytes 2097152 | tf_op jit(solution)/shard_map/all_to_all | solution.py:34
  51.1 1.9 copy.118
  53.0 4.0 %fusion.9 = f32[3,8,128,128]{2,3,0,1:T(8,128)} fusion(f32[512,8,128]{0,2,1:T(8,128)} %copy.118, f32[3,512,8]{1,0,2:T(4,128)S(1)} %copy.99, bf16[512,8,128,1]{2,1,0,3:T(8,128)(2,1)} %bitcast.136), kind=kOutput, calls=%fused_computation.19 | convolution fusion | flops 405798912 | bytes 4767744 | tf_op jit(solution)/shard_map/phd,bphe->bhde/dot_general | solution.py:65
  57.0 2.0 copy.120
  59.0 4.4 %fusion.53 = f32[8,8,128,128]{3,0,2,1:T(8,128)S(1)} fusion(f32[3,8,128,128]{3,0,2,1:T(4,128)S(1)} %copy.120, f32[8,1]{0,1:T(1,128)S(1)} %and_select_fusion, f32[8,1]{0,1:T(1,128)S(1)} %and_select_fusion.3, f32[8,1]{0,1:T(1,128)S(1)} %and_select_fusion.6), kind=kOutput, calls=%fused_computation.129 | convolution fusion | flops 37748784 | bytes 5767264 | tf_op jit(solution)/shard_map/tb,bhde->thde/dot_general | solution.py:82
  63.4 2.7 %copy.121 = f32[8,8,128,128]{3,2,1,0:T(8,128)} copy(f32[8,8,128,128]{3,0,2,1:T(8,128)S(1)} %fusion.53) | data formatting | bytes 8388608 | tf_op jit(solution)/shard_map/tb,bhde->thde/dot_general | solution.py:82
  68.4 3.7 %all-to-all-start.2 = ((bf16[128,4,1024]{2,0,1:T(8,128)(2,1)}), bf16[128,4,1024]{2,0,1:T(8,128)(2,1)S(1)}, u32[]{:S(2)}, u32[]{:S(2)}) async-start(bf16[128,4,1024]{2,0,1:T(8,128)(2,1)} %bitcast.121), calls=%async_computation.2 | async-start | bytes 2097152 | tf_op jit(solution)/shard_map/all_to_all | solution.py:35
  72.3 1.5 copy.159
  73.8 12.7 %all-to-all-done.2 = bf16[128,4,1024]{2,0,1:T(8,128)(2,1)S(1)} async-done(((bf16[128,4,1024]{2,0,1:T(8,128)(2,1)}), bf16[128,4,1024]{2,0,1:T(8,128)(2,1)S(1)}, u32[]{:S(2)}, u32[]{:S(2)}) %all-to-all-start.2) | async-done | bytes 1048608 | tf_op jit(solution)/shard_map/all_to_all | solution.py:35
  87.4 1.5 copy.160
  89.6 2.3 collective-permute-start
  91.9 3.0 %broadcast_compare_fusion.9 = (pred[512,512]{1,0:T(8,128)(4,1)S(1)}, pred[512,512]{1,0:T(8,128)(4,1)S(1)}, pred[512,512]{1,0:T(8,128)(4,1)S(1)}, pred[512,512]{1...) fusion(s32[512]{0:T(512)S(1)} %get-tuple-element.72, ...), kind=kLoop, calls=%fused_computation.60 | loop fusion | flops 9437184 | bytes 2637824 | tf_op jit(solution)/shard_map/while/body/eval_jaxpr/eq | solution.py:106
  94.9 14.3 %collective-permute-done = f32[8,128,128]{2,1,0:T(8,128)S(1)} collective-permute-done((f32[8,128,128]{2,1,0:T(8,128)S(1)}, f32[8,128,128]{2,1,0:T(8,128)S(1)}, u32[]{:S(2)}, u32[]{:S(2)}) %collective-permute-start) | collective-permute-done | bytes 524320 | tf_op jit(solution)/shard_map/ppermute | solution.py:14
  109.4 2.1 collective-permute-start.1
  111.5 10.5 %multiply_convert_fusion = bf16[8,512,512]{2,1,0:T(8,128)(2,1)} fusion(f32[8,512]{1,0:T(8,128)S(1)} %get-tuple-element.53, f32[8,512]{1,0:T(8,128)S(1)} %get-tuple-element.54, f32[8,512]{1,0:T(8,128)S(1)} %copy-done.9, f32[8,512]{1,0:T(8,128)S(1)} %copy-done.10, f32[8,512]{1,0:T(8,128)S(1)} %copy-done.11, f32[8,512]{1,0:T(8,128)S(1)} %copy-done.12, ...), kind=kOutput, calls=%fused_computation | convolution fusion | flops 566231040 | bytes 9338880 | tf_op jit(solution)/shard_map/while/body/eval_jaxpr/phe,she->hps/dot_general | solution.py:118
  122.0 3.7 %collective-permute-done.1 = f32[8,128,128]{2,1,0:T(8,128)S(1)} collective-permute-done((f32[8,128,128]{2,1,0:T(8,128)S(1)}, f32[8,128,128]{2,1,0:T(8,128)S(1)}, u32[]{:S(2)}, u32[]{:S(2)}) %collective-permute-start.1) | collective-permute-done | bytes 524320 | tf_op jit(solution)/shard_map/ppermute | solution.py:14
  125.8 1.6 collective-permute-start.2
  127.5 10.5 %multiply_convert_fusion.1 = bf16[8,512,512]{2,1,0:T(8,128)(2,1)} fusion(f32[8,512]{1,0:T(8,128)S(1)} %get-tuple-element.53, f32[8,512]{1,0:T(8,128)S(1)} %get-tuple-element.54, f32[8,512]{1,0:T(8,128)S(1)} %copy-done.9, f32[8,512]{1,0:T(8,128)S(1)} %copy-done.10, f32[8,512]{1,0:T(8,128)S(1)} %copy-done.11, f32[8,512]{1,0:T(8,128)S(1)} %copy-done.12, ...), kind=kOutput, calls=%fused_computation.1 | convolution fusion | flops 566231040 | bytes 9338880 | tf_op jit(solution)/shard_map/while/body/eval_jaxpr/phd,shd->hps/dot_general | solution.py:111
  137.9 30.2 %collective-permute-done.2 = f32[8,128,128]{2,1,0:T(8,128)S(1)} collective-permute-done((f32[8,128,128]{2,1,0:T(8,128)S(1)}, f32[8,128,128]{2,1,0:T(8,128)S(1)}, u32[]{:S(2)}, u32[]{:S(2)}) %collective-permute-start.2) | collective-permute-done | bytes 524320 | tf_op jit(solution)/shard_map/ppermute | solution.py:14
  168.9 2.3 fusion
  171.2 2.9 %copy.113 = f32[512,8,128]{2,0,1:T(8,128)} copy(f32[512,8,128]{0,2,1:T(8,128)} %fusion) | data formatting | bytes 4194304 | tf_op jit(solution)/shard_map/reduce_sum | solution.py:144
  174.1 4.1 %fusion.7 = bf16[512,8,128]{2,0,1:T(8,128)(2,1)S(1)} fusion(f32[512,8,128]{2,0,1:T(8,128)} %copy.113, bf16[8,512,512]{2,1,0:T(8,128)(2,1)} %multiply_convert_fusion, bf16[512,8,128]{2,1,0:T(8,128)(2,1)S(1)} %bitcast.130), kind=kOutput, calls=%fused_computation.16 | convolution fusion | flops 537919488 | bytes 8388608 | tf_op jit(solution)/shard_map/while/body/eval_jaxpr/hps,shd->phd/dot_general | solution.py:122
  178.2 1.6 copy.114
  179.9 2.3 convert_element_type.558
  182.1 4.5 %all-to-all-start.5 = ((bf16[4,128,1024]{2,1,0:T(8,128)(2,1)}), bf16[4,128,1024]{2,1,0:T(8,128)(2,1)}, u32[]{:S(2)}, u32[]{:S(2)}) async-start(bf16[4,128,1024]{2,1,0:T(8,128)(2,1)} %convert_element_type.558), calls=%async_computation.5 | async-start | bytes 2097152 | tf_op jit(solution)/shard_map/all_to_all | solution.py:172
  186.6 3.9 %fusion.1 = f32[512,8,128]{0,2,1:T(8,128)} fusion(f32[3,512,8]{1,0,2:T(4,128)S(1)} %copy.99, bf16[512,8,128,1]{2,1,0,3:T(8,128)(2,1)} %bitcast.137, bf16[1,8,128,128]{3,2,1,0:T(8,128)(2,1)} %copy-done.8, bf16[1,8,128,128]{3,2,1,0:T(8,128)(2,1)} %copy-done.7, bf16[1,8,128,128]{3,2,1,0:T(8,128)(2,1)S(1)} %copy-done.6), kind=kOutput, calls=%fused_computation.6 | convolution fusion | flops 406061056 | bytes 3981312 | tf_op jit(solution)/shard_map/phd,bhde->bphe/dot_general | solution.py:141
  190.5 2.9 %copy.104 = f32[512,8,128]{2,0,1:T(8,128)} copy(f32[512,8,128]{0,2,1:T(8,128)} %fusion.1) | data formatting | bytes 4194304 | tf_op jit(solution)/shard_map/reduce_sum | solution.py:139
  193.4 4.1 %fusion.8 = bf16[512,8,128]{2,0,1:T(8,128)(2,1)S(1)} fusion(f32[512,8,128]{2,0,1:T(8,128)} %copy.104, bf16[8,512,512]{2,1,0:T(8,128)(2,1)} %multiply_convert_fusion.1, bf16[512,8,128]{2,1,0:T(8,128)(2,1)S(1)} %bitcast.134), kind=kOutput, calls=%fused_computation.18 | convolution fusion | flops 537919488 | bytes 8388608 | tf_op jit(solution)/shard_map/while/body/eval_jaxpr/hps,she->phe/dot_general | solution.py:115
  197.6 1.6 copy.105
  199.2 2.3 convert_element_type.555
  201.5 4.3 %all-to-all-start.3 = ((bf16[4,128,1024]{2,1,0:T(8,128)(2,1)}), bf16[4,128,1024]{2,1,0:T(8,128)(2,1)}, u32[]{:S(2)}, u32[]{:S(2)}) async-start(bf16[4,128,1024]{2,1,0:T(8,128)(2,1)} %convert_element_type.555), calls=%async_computation.3 | async-start | bytes 2097152 | tf_op jit(solution)/shard_map/all_to_all | solution.py:171
  205.8 5.2 %fusion.16 = f32[8,512,128]{2,1,0:T(8,128)} fusion(bf16[8,512,512]{2,1,0:T(8,128)(2,1)} %multiply_convert_fusion, bf16[512,8,128]{2,1,0:T(8,128)(2,1)} %bitcast.138), kind=kOutput, calls=%fused_computation.33 | convolution fusion | flops 536870912 | bytes 7340032 | tf_op jit(solution)/shard_map/while/body/eval_jaxpr/hps,phd->shd/dot_general | solution.py:125
  212.1 2.0 fusion.6
  216.1 4.2 %all-to-all-done.3 = bf16[4,128,1024]{2,1,0:T(8,128)(2,1)} async-done(((bf16[4,128,1024]{2,1,0:T(8,128)(2,1)}), bf16[4,128,1024]{2,1,0:T(8,128)(2,1)}, u32[]{:S(2)}, u32[]{:S(2)}) %all-to-all-start.3) | async-done | bytes 1048608 | tf_op jit(solution)/shard_map/all_to_all | solution.py:171
  220.3 3.5 %all-to-all-start.6 = ((bf16[4,128,1024]{2,1,0:T(8,128)(2,1)}), bf16[4,128,1024]{2,1,0:T(8,128)(2,1)S(1)}, u32[]{:S(2)}, u32[]{:S(2)}) async-start(bf16[4,128,1024]{2,1,0:T(8,128)(2,1)} %all_to_all.118), calls=%async_computation.7 | async-start | bytes 2097152 | tf_op jit(solution)/shard_map/all_to_all | solution.py:173
  223.8 3.6 %fusion.13 = f32[8,512,128]{2,1,0:T(8,128)S(1)} fusion(bf16[8,512,512]{2,1,0:T(8,128)(2,1)} %multiply_convert_fusion.1, bf16[512,8,128]{2,1,0:T(8,128)(2,1)S(1)} %bitcast.127), kind=kOutput, calls=%fused_computation.30 | convolution fusion | flops 536870912 | bytes 7340032 | tf_op jit(solution)/shard_map/while/body/eval_jaxpr/hps,phe->she/dot_general | solution.py:128
  229.8 8.4 %all-to-all-done.6 = bf16[4,128,1024]{2,1,0:T(8,128)(2,1)S(1)} async-done(((bf16[4,128,1024]{2,1,0:T(8,128)(2,1)}), bf16[4,128,1024]{2,1,0:T(8,128)(2,1)S(1)}, u32[]{:S(2)}, u32[]{:S(2)}) %all-to-all-start.6) | async-done | bytes 1048608 | tf_op jit(solution)/shard_map/all_to_all | solution.py:173
  238.2 3.5 %all-to-all-start.7 = ((bf16[4,128,1024]{2,1,0:T(8,128)(2,1)}), bf16[4,128,1024]{2,1,0:T(8,128)(2,1)S(1)}, u32[]{:S(2)}, u32[]{:S(2)}) async-start(bf16[4,128,1024]{2,1,0:T(8,128)(2,1)} %all_to_all.122), calls=%async_computation.8 | async-start | bytes 2097152 | tf_op jit(solution)/shard_map/all_to_all | solution.py:174
  241.7 1.6 copy.115
  243.3 1.3 copy.134
  244.6 1.6 copy.106
  246.3 1.3 copy.133
  249.5 6.6 %all-to-all-done.7 = bf16[4,128,1024]{2,1,0:T(8,128)(2,1)S(1)} async-done(((bf16[4,128,1024]{2,1,0:T(8,128)(2,1)}), bf16[4,128,1024]{2,1,0:T(8,128)(2,1)S(1)}, u32[]{:S(2)}, u32[]{:S(2)}) %all-to-all-start.7) | async-done | bytes 1048608 | tf_op jit(solution)/shard_map/all_to_all | solution.py:174
  (69 shorter events, 19.8 us)
Async XLA Ops:
  7.2 6.8 %copy-start.2 = (bf16[128,4096]{1,0:T(8,128)(2,1)S(1)}, bf16[128,4096]{1,0:T(8,128)(2,1)}, u32[]{:S(2)}) copy-start(bf16[128,4096]{1,0:T(8,128)(2,1)} %param.8) | copy-start | bytes 3145732
  9.5 24.1 %copy-start.3 = (bf16[128,4096]{1,0:T(8,128)(2,1)S(1)}, bf16[128,4096]{1,0:T(8,128)(2,1)}, u32[]{:S(2)}) copy-start(bf16[128,4096]{1,0:T(8,128)(2,1)} %param.6) | copy-start | bytes 3145732
  9.5 18.8 %all-to-all-start = ((bf16[128,4,1024]{2,0,1:T(8,128)(2,1)}), bf16[128,4,1024]{2,0,1:T(8,128)(2,1)S(1)}, u32[]{:S(2)}, u32[]{:S(2)}) async-start(bf16[128,4,1024]{2,0,1:T(8,128)(2,1)} %bitcast.123), calls=%async_computation | async-start | bytes 2097152 | tf_op jit(solution)/shard_map/all_to_all | solution.py:33
  28.3 17.9 %all-to-all-start.4 = ((bf16[128,4,1024]{2,0,1:T(8,128)(2,1)}), bf16[128,4,1024]{2,0,1:T(8,128)(2,1)S(1)}, u32[]{:S(2)}, u32[]{:S(2)}) async-start(bf16[128,4,1024]{2,0,1:T(8,128)(2,1)} %bitcast.120), calls=%async_computation.4 | async-start | bytes 2097152 | tf_op jit(solution)/shard_map/all_to_all | solution.py:36
  46.3 22.1 %all-to-all-start.1 = ((bf16[128,4,1024]{2,0,1:T(8,128)(2,1)}), bf16[128,4,1024]{2,0,1:T(8,128)(2,1)}, u32[]{:S(2)}, u32[]{:S(2)}) async-start(bf16[128,4,1024]{2,0,1:T(8,128)(2,1)} %bitcast.122), calls=%async_computation.1 | async-start | bytes 2097152 | tf_op jit(solution)/shard_map/all_to_all | solution.py:34
  50.5 160.5 %reduce-scatter.2.cloned.1.call-start = ((), (), s32[]{:S(2)}) async-start(), calls=%async_computation.9 | async-start | bytes 4718592 | tf_op jit(solution)/shard_map/reduce_scatter | solution.py:83
  66.1 1.2 copy-start.4
  68.4 18.0 %all-to-all-start.2 = ((bf16[128,4,1024]{2,0,1:T(8,128)(2,1)}), bf16[128,4,1024]{2,0,1:T(8,128)(2,1)S(1)}, u32[]{:S(2)}, u32[]{:S(2)}) async-start(bf16[128,4,1024]{2,0,1:T(8,128)(2,1)} %bitcast.121), calls=%async_computation.2 | async-start | bytes 2097152 | tf_op jit(solution)/shard_map/all_to_all | solution.py:35
  86.4 1.0 copy-start.1
  88.9 22.5 %copy-start.9 = (f32[8,512]{1,0:T(8,128)S(1)}, f32[8,512]{1,0:T(8,128)}, u32[]{:S(2)}) copy-start(f32[8,512]{1,0:T(8,128)} %get-tuple-element.55) | copy-start | bytes 49156
  88.9 22.5 %copy-start.10 = (f32[8,512]{1,0:T(8,128)S(1)}, f32[8,512]{1,0:T(8,128)}, u32[]{:S(2)}) copy-start(f32[8,512]{1,0:T(8,128)} %get-tuple-element.56) | copy-start | bytes 49156
  88.9 22.5 %copy-start.11 = (f32[8,512]{1,0:T(8,128)S(1)}, f32[8,512]{1,0:T(8,128)}, u32[]{:S(2)}) copy-start(f32[8,512]{1,0:T(8,128)} %get-tuple-element.57) | copy-start | bytes 49156
  88.9 22.5 %copy-start.12 = (f32[8,512]{1,0:T(8,128)S(1)}, f32[8,512]{1,0:T(8,128)}, u32[]{:S(2)}) copy-start(f32[8,512]{1,0:T(8,128)} %get-tuple-element.58) | copy-start | bytes 49156
  89.0 22.5 %copy-start.13 = (f32[8,512]{1,0:T(8,128)S(1)}, f32[8,512]{1,0:T(8,128)}, u32[]{:S(2)}) copy-start(f32[8,512]{1,0:T(8,128)} %get-tuple-element.59) | copy-start | bytes 49156
  89.0 22.5 %copy-start.14 = (f32[8,512]{1,0:T(8,128)S(1)}, f32[8,512]{1,0:T(8,128)}, u32[]{:S(2)}) copy-start(f32[8,512]{1,0:T(8,128)} %get-tuple-element.60) | copy-start | bytes 49156
  89.0 22.5 %copy-start.15 = (f32[8,512]{1,0:T(8,128)S(1)}, f32[8,512]{1,0:T(8,128)}, u32[]{:S(2)}) copy-start(f32[8,512]{1,0:T(8,128)} %get-tuple-element.61) | copy-start | bytes 49156
  89.6 19.7 %collective-permute-start = (f32[8,128,128]{2,1,0:T(8,128)S(1)}, f32[8,128,128]{2,1,0:T(8,128)S(1)}, u32[]{:S(2)}, u32[]{:S(2)}) collective-permute-start(f32[8,128,128]{2,1,0:T(8,128)S(1)} %fusion.23), channel_id=1, source_target_pairs={{0,4},{4,0},{8,12},{12,8},{16,20},{20,16},{24,28},{28,24},{1,5},{5... | collective-permute-start | bytes 1572872 | tf_op jit(solution)/shard_map/ppermute | solution.py:14
  109.4 58.8 %copy-start.5 = (bf16[1,8,128,128]{3,2,1,0:T(8,128)(2,1)}, bf16[1,8,128,128]{3,2,1,0:T(8,128)(2,1)S(1)}, u32[]{:S(2)}) copy-start(bf16[1,8,128,128]{3,2,1,0:T(8,128)(2,1)S(1)} %get-tuple-element.45) | copy-start | bytes 786436
  109.4 16.4 %collective-permute-start.1 = (f32[8,128,128]{2,1,0:T(8,128)S(1)}, f32[8,128,128]{2,1,0:T(8,128)S(1)}, u32[]{:S(2)}, u32[]{:S(2)}) collective-permute-start(f32[8,128,128]{2,1,0:T(8,128)S(1)} %get-tuple-element.46), channel_id=1, source_target_pairs={{0,8},{8,0},{4,12},{12,4},{16,24},{24,16},{20,28},{28,20},{1,9},{9... | collective-permute-start | bytes 1572872 | tf_op jit(solution)/shard_map/ppermute | solution.py:14
  111.5 16.0 %copy-start = (bf16[64,8,8,128]{3,2,1,0:T(8,128)(2,1)S(1)}, bf16[64,8,8,128]{3,2,1,0:T(8,128)(2,1)}, u32[]{:S(2)}) copy-start(bf16[64,8,8,128]{3,2,1,0:T(8,128)(2,1)} %copy.158) | copy-start | bytes 3145732
  125.8 42.4 %copy-start.7 = (bf16[1,8,128,128]{3,2,1,0:T(8,128)(2,1)}, bf16[1,8,128,128]{3,2,1,0:T(8,128)(2,1)S(1)}, u32[]{:S(2)}) copy-start(bf16[1,8,128,128]{3,2,1,0:T(8,128)(2,1)S(1)} %get-tuple-element.47) | copy-start | bytes 786436
  125.8 42.3 %collective-permute-start.2 = (f32[8,128,128]{2,1,0:T(8,128)S(1)}, f32[8,128,128]{2,1,0:T(8,128)S(1)}, u32[]{:S(2)}, u32[]{:S(2)}) collective-permute-start(f32[8,128,128]{2,1,0:T(8,128)S(1)} %get-tuple-element.48), channel_id=1, source_target_pairs={{0,16},{16,0},{4,20},{20,4},{8,24},{24,8},{12,28},{28,12},{1,17},{... | collective-permute-start | bytes 1572872 | tf_op jit(solution)/shard_map/ppermute | solution.py:14
  168.2 0.7 copy-start.8
  178.2 8.4 %copy-start.6 = (bf16[1,8,128,128]{3,2,1,0:T(8,128)(2,1)S(1)}, bf16[1,8,128,128]{3,2,1,0:T(8,128)(2,1)}, u32[]{:S(2)}) copy-start(bf16[1,8,128,128]{3,2,1,0:T(8,128)(2,1)} %copy-done.5) | copy-start | bytes 786436
  182.1 19.4 %all-to-all-start.5 = ((bf16[4,128,1024]{2,1,0:T(8,128)(2,1)}), bf16[4,128,1024]{2,1,0:T(8,128)(2,1)}, u32[]{:S(2)}, u32[]{:S(2)}) async-start(bf16[4,128,1024]{2,1,0:T(8,128)(2,1)} %convert_element_type.558), calls=%async_computation.5 | async-start | bytes 2097152 | tf_op jit(solution)/shard_map/all_to_all | solution.py:172
  201.5 18.8 %all-to-all-start.3 = ((bf16[4,128,1024]{2,1,0:T(8,128)(2,1)}), bf16[4,128,1024]{2,1,0:T(8,128)(2,1)}, u32[]{:S(2)}, u32[]{:S(2)}) async-start(bf16[4,128,1024]{2,1,0:T(8,128)(2,1)} %convert_element_type.555), calls=%async_computation.3 | async-start | bytes 2097152 | tf_op jit(solution)/shard_map/all_to_all | solution.py:171
  220.3 17.9 %all-to-all-start.6 = ((bf16[4,128,1024]{2,1,0:T(8,128)(2,1)}), bf16[4,128,1024]{2,1,0:T(8,128)(2,1)S(1)}, u32[]{:S(2)}, u32[]{:S(2)}) async-start(bf16[4,128,1024]{2,1,0:T(8,128)(2,1)} %all_to_all.118), calls=%async_computation.7 | async-start | bytes 2097152 | tf_op jit(solution)/shard_map/all_to_all | solution.py:173
  238.2 17.9 %all-to-all-start.7 = ((bf16[4,128,1024]{2,1,0:T(8,128)(2,1)}), bf16[4,128,1024]{2,1,0:T(8,128)(2,1)S(1)}, u32[]{:S(2)}, u32[]{:S(2)}) async-start(bf16[4,128,1024]{2,1,0:T(8,128)(2,1)} %all_to_all.122), calls=%async_computation.8 | async-start | bytes 2097152 | tf_op jit(solution)/shard_map/all_to_all | solution.py:174
Sparse Core Ops, SparseCore 0:
  66.3 102.7 reduce-scatter.1
where the time goes:
time: 266 us; the launch traced here: 265 us
  waiting for transfers between devices  104 us (39%)
  matrix products  55.8 us (21%)
  local copies, waits for them, and re-layouts  46.9 us (18%)
  starting transfers between devices  37.6 us (14%)
  between operations  14.6 us (5%)
  other arithmetic  6.23 us (2%)
    ppermute x3, waiting for transfers between devices, swapped(): return lax.ppermute(block, axis, route)  48.2 us
    all_to_all x1, waiting for transfers between devices, on_device(): lax.all_to_all(query_input, 'head', split_axis=1, concat_axis=0, tiled=True)  13.4 us
    all_to_all x1, waiting for transfers between devices, on_device(): lax.all_to_all(value_input, 'head', split_axis=1, concat_axis=0, tiled=True)  12.7 us
    unnamed x40, local copies, waits for them, and re-layouts  12.7 us
    dot_general x1, matrix products, row_step(): jnp.einsum('phe,she->hps', cot_heads, value_heads, preferred_element_type...  10.5 us
    dot_general x1, matrix products, row_step(): jnp.einsum('phd,shd->hps', query_heads, key_heads, preferred_element_type...  10.5 us
    all_to_all x1, waiting for transfers between devices, on_device(): lax.all_to_all(cotangent, 'head', split_axis=1, concat_axis=0, tiled=True)  10.3 us
    all_to_all x1, waiting for transfers between devices, on_device(): lax.all_to_all(grad_key, 'head', split_axis=0, concat_axis=1, tiled=True)  8.37 us
  transfers between devices with their start and end apart: 12, of which 9 were waited for; matrix products, arithmetic and copies ran while one was open for 37% of the time, Pallas kernels for 0%

commit v1 on v0

--- a/solution.py
+++ b/solution.py
@@ -2,6 +2,22 @@
 import jax.numpy as jnp
 from jax import lax
 from jax.sharding import PartitionSpec as P
+
+
+def swapped_with_each(shard, axis, split, join):
+    ways, here = (lax.axis_size(axis), lax.axis_index(axis))
+    width = shard.shape[split] // ways
+    lengths = list(shard.shape)
+    lengths[split] = width
+    height = lengths[join]
+    lengths[join] = height * ways
+    full = jnp.zeros(lengths, shard.dtype)
+    for mask in range(ways):
+        part = lax.dynamic_slice_in_dim(shard, (here ^ mask) * width, width, axis=split)
+        if mask:
+            part = lax.ppermute(part, axis, [(d, d ^ mask) for d in range(ways)])
+        full = lax.dynamic_update_slice_in_dim(full, part, (here ^ mask) * height, axis=join)
+    return full
 
 
 def swapped(block, axis, stride):
@@ -33,7 +49,7 @@
         lax.all_to_all(query_input, "head", split_axis=1, concat_axis=0, tiled=True),
         lax.all_to_all(key_input, "head", split_axis=1, concat_axis=0, tiled=True),
         lax.all_to_all(value_input, "head", split_axis=1, concat_axis=0, tiled=True),
-        lax.all_to_all(cotangent, "head", split_axis=1, concat_axis=0, tiled=True),
+        swapped_with_each(cotangent, "head", 1, 0),
     )
     head_count = level_codes.shape[0]
     total_levels = level_codes.shape[1]

time: 266 us -> 253 us (0.951)
  waiting for transfers between devices: 104 us -> 89.5 us
  matrix products: 55.8 us -> 48.7 us
  local copies, waits for them, and re-layouts: 46.9 us -> 52.7 us
  other arithmetic: 6.23 us -> 9.92 us
    all_to_all x1 -> x0, waiting for transfers between devices: 10.3 us -> none  [on_device(): lax.all_to_all(cotangent, 'head', split_axis=1, concat_axis=0, tiled=True)]
    ppermute x3, waiting for transfers between devices: 48.2 us -> 43.9 us  [swapped(): return lax.ppermute(block, axis, route)]
    all_to_all x1, waiting for transfers between devices: 13.4 us -> 9.36 us  [on_device(): lax.all_to_all(query_input, 'head', split_axis=1, concat_axis=0, tiled=True)]
    all_to_all x1, waiting for transfers between devices: 4.18 us -> 7.82 us  [on_device(): lax.all_to_all(attended, 'head', split_axis=0, concat_axis=1, tiled=True)]
    all_to_all x1 -> x0, starting transfers between devices: 3.52 us -> none  [on_device(): lax.all_to_all(cotangent, 'head', split_axis=1, concat_axis=0, tiled=True)]
    ppermute x0 -> x3, starting transfers between devices: none -> 3.08 us  [swapped_with_each(): part = lax.ppermute(part, axis, [(d, d ^ mask) for d in range(ways)])]
    unnamed x40 -> x49, local copies, waits for them, and re-layouts: 12.7 us -> 15 us
  transfers between devices with their start and end apart: 12 -> 14, of which waited for: 9 -> 9; matrix products, arithmetic and copies ran while one was open for 37% -> 39% of each run, Pallas kernels for 0% -> 0%
where the time goes in v1:
time: 253 us; the launch traced here: 251 us
  waiting for transfers between devices  89.5 us (35%)
  local copies, waits for them, and re-layouts  52.7 us (21%)
  matrix products  48.7 us (19%)
  starting transfers between devices  35.9 us (14%)
  between operations  14.7 us (6%)
  other arithmetic  9.92 us (4%)
    ppermute x3, waiting for transfers between devices, swapped(): return lax.ppermute(block, axis, route)  43.9 us
    unnamed x49, local copies, waits for them, and re-layouts  15 us
    all_to_all x1, waiting for transfers between devices, on_device(): lax.all_to_all(value_input, 'head', split_axis=1, concat_axis=0, tiled=True)  12.7 us
    dot_general x1, matrix products, row_step(): jnp.einsum('phd,shd->hps', query_heads, key_heads, preferred_element_type...  10.6 us
    dot_general x1, matrix products, row_step(): jnp.einsum('phe,she->hps', cot_heads, value_heads, preferred_element_type...  10 us
    all_to_all x1, waiting for transfers between devices, on_device(): lax.all_to_all(query_input, 'head', split_axis=1, concat_axis=0, tiled=True)  9.36 us
    all_to_all x1, waiting for transfers between devices, on_device(): lax.all_to_all(grad_value, 'head', split_axis=0, concat_axis=1, tiled=True)  8.35 us
    all_to_all x1, waiting for transfers between devices, on_device(): lax.all_to_all(attended, 'head', split_axis=0, concat_axis=1, tiled=True)  7.82 us
  transfers between devices with their start and end apart: 14, of which 9 were waited for; matrix products, arithmetic and copies ran while one was open for 39% of the time, Pallas kernels for 0%

profile of v1, /device:TPU:0, one launch (start us, length us, event | category | flops | bytes accessed | tf_op | source)
XLA Modules:
  0.0 251.4 jit_solution(4446103981617654276)
XLA Ops:
  7.3 2.1 constant_dynamic-slice_fusion
  9.9 2.5 collective-permute-start.4
  12.5 2.3 copy.190
  14.8 3.5 %all-to-all-start = ((bf16[128,4,1024]{2,0,1:T(8,128)(2,1)}), bf16[128,4,1024]{2,0,1:T(8,128)(2,1)S(1)}, u32[]{:S(2)}, u32[]{:S(2)}) async-start(bf16[128,4,1024]{2,0,1:T(8,128)(2,1)} %bitcast.119), calls=%async_computation | async-start | bytes 2097152 | tf_op jit(solution)/shard_map/all_to_all | solution.py:49
  20.3 2.3 copy.189
  25.4 1.6 convert_element_type.562
  27.1 9.4 %all-to-all-done = bf16[128,4,1024]{2,0,1:T(8,128)(2,1)S(1)} async-done(((bf16[128,4,1024]{2,0,1:T(8,128)(2,1)}), bf16[128,4,1024]{2,0,1:T(8,128)(2,1)S(1)}, u32[]{:S(2)}, u32[]{:S(2)}) %all-to-all-start) | async-done | bytes 1048608 | tf_op jit(solution)/shard_map/all_to_all | solution.py:49
  36.4 4.3 %all-to-all-start.1 = ((bf16[128,4,1024]{2,0,1:T(8,128)(2,1)}), bf16[128,4,1024]{2,0,1:T(8,128)(2,1)}, u32[]{:S(2)}, u32[]{:S(2)}) async-start(bf16[128,4,1024]{2,0,1:T(8,128)(2,1)} %bitcast.118), calls=%async_computation.1 | async-start | bytes 2097152 | tf_op jit(solution)/shard_map/all_to_all | solution.py:50
  42.0 3.7 %fusion.8 = f32[3,8,128,128]{2,3,0,1:T(8,128)} fusion(f32[512,8,128]{0,2,1:T(8,128)} %convert_element_type.562, f32[3,512,8]{1,0,2:T(4,128)S(1)} %copy.99, bf16[512,8,128,1]{2,1,0,3:T(8,128)(2,1)S(1)} %bitcast.133), kind=kOutput, calls=%fused_computation.18 | convolution fusion | flops 405798912 | bytes 4767744 | tf_op jit(solution)/shard_map/phd,bphe->bhde/dot_general | solution.py:81
  45.7 2.0 copy.122
  47.7 4.4 %fusion.51 = f32[8,8,128,128]{3,0,2,1:T(8,128)S(1)} fusion(f32[3,8,128,128]{3,0,2,1:T(4,128)S(1)} %copy.122, f32[8,1]{0,1:T(1,128)S(1)} %and_select_fusion, f32[8,1]{0,1:T(1,128)S(1)} %copy-done.20, f32[8,1]{0,1:T(1,128)S(1)} %and_select_fusion.6), kind=kOutput, calls=%fused_computation.127 | convolution fusion | flops 37748784 | bytes 5767264 | tf_op jit(solution)/shard_map/tb,bhde->thde/dot_general | solution.py:98
  52.2 2.7 %copy.123 = f32[8,8,128,128]{3,2,1,0:T(8,128)} copy(f32[8,8,128,128]{3,0,2,1:T(8,128)S(1)} %fusion.51) | data formatting | bytes 8388608 | tf_op jit(solution)/shard_map/tb,bhde->thde/dot_general | solution.py:98
  57.2 3.7 %all-to-all-start.2 = ((bf16[128,4,1024]{2,0,1:T(8,128)(2,1)}), bf16[128,4,1024]{2,0,1:T(8,128)(2,1)S(1)}, u32[]{:S(2)}, u32[]{:S(2)}) async-start(bf16[128,4,1024]{2,0,1:T(8,128)(2,1)} %bitcast.117), calls=%async_computation.2 | async-start | bytes 2097152 | tf_op jit(solution)/shard_map/all_to_all | solution.py:51
  61.0 1.5 copy.155
  62.5 12.7 %all-to-all-done.2 = bf16[128,4,1024]{2,0,1:T(8,128)(2,1)S(1)} async-done(((bf16[128,4,1024]{2,0,1:T(8,128)(2,1)}), bf16[128,4,1024]{2,0,1:T(8,128)(2,1)S(1)}, u32[]{:S(2)}, u32[]{:S(2)}) %all-to-all-start.2) | async-done | bytes 1048608 | tf_op jit(solution)/shard_map/all_to_all | solution.py:51
  76.2 1.5 copy.156
  78.4 1.8 collective-permute-start
  80.2 3.0 %broadcast_compare_fusion.9 = (pred[512,512]{1,0:T(8,128)(4,1)S(1)}, pred[512,512]{1,0:T(8,128)(4,1)S(1)}, pred[512,512]{1,0:T(8,128)(4,1)S(1)}, pred[512,512]{1...) fusion(s32[512]{0:T(512)S(1)} %get-tuple-element.76, ...), kind=kLoop, calls=%fused_computation.57 | loop fusion | flops 9437184 | bytes 2637824 | tf_op jit(solution)/shard_map/while/body/eval_jaxpr/eq | solution.py:122
  83.2 14.3 %collective-permute-done = f32[8,128,128]{2,1,0:T(8,128)S(1)} collective-permute-done((f32[8,128,128]{2,1,0:T(8,128)S(1)}, f32[8,128,128]{2,1,0:T(8,128)S(1)}, u32[]{:S(2)}, u32[]{:S(2)}) %collective-permute-start) | collective-permute-done | bytes 524320 | tf_op jit(solution)/shard_map/ppermute | solution.py:30
  97.7 2.1 collective-permute-start.1
  99.8 10.6 %multiply_convert_fusion.1 = bf16[8,512,512]{2,1,0:T(8,128)(2,1)} fusion(f32[8,512]{1,0:T(8,128)S(1)} %get-tuple-element.57, f32[8,512]{1,0:T(8,128)S(1)} %copy-done.12, f32[8,512]{1,0:T(8,128)S(1)} %copy-done.13, f32[8,512]{1,0:T(8,128)S(1)} %copy-done.14, f32[8,512]{1,0:T(8,128)S(1)} %copy-done.15, f32[8,512]{1,0:T(8,128)S(1)} %copy-done.16, ...), kind=kOutput, calls=%fused_computation.1 | convolution fusion | flops 566231040 | bytes 9338880 | tf_op jit(solution)/shard_map/while/body/eval_jaxpr/phd,shd->hps/dot_general | solution.py:127
  110.4 3.5 %collective-permute-done.1 = f32[8,128,128]{2,1,0:T(8,128)S(1)} collective-permute-done((f32[8,128,128]{2,1,0:T(8,128)S(1)}, f32[8,128,128]{2,1,0:T(8,128)S(1)}, u32[]{:S(2)}, u32[]{:S(2)}) %collective-permute-start.1) | collective-permute-done | bytes 524320 | tf_op jit(solution)/shard_map/ppermute | solution.py:30
  114.0 1.6 collective-permute-start.2
  115.7 10.0 %multiply_convert_fusion = bf16[8,512,512]{2,1,0:T(8,128)(2,1)S(1)} fusion(f32[8,512]{1,0:T(8,128)S(1)} %get-tuple-element.57, f32[8,512]{1,0:T(8,128)S(1)} %copy-done.12, f32[8,512]{1,0:T(8,128)S(1)} %copy-done.13, f32[8,512]{1,0:T(8,128)S(1)} %copy-done.14, f32[8,512]{1,0:T(8,128)S(1)} %copy-done.15, f32[8,512]{1,0:T(8,128)S(1)} %copy-done.16, ...), kind=kOutput, calls=%fused_computation | convolution fusion | flops 566231040 | bytes 9338880 | tf_op jit(solution)/shard_map/while/body/eval_jaxpr/phe,she->hps/dot_general | solution.py:134
  125.7 2.0 copy-done
  127.7 2.6 %fusion.25 = f32[8,512,128]{2,1,0:T(8,128)} fusion(bf16[8,512,512]{2,1,0:T(8,128)(2,1)S(1)} %multiply_convert_fusion, bf16[512,8,128]{2,1,0:T(8,128)(2,1)S(1)} %bitcast.123), kind=kOutput, calls=%fused_computation.42 | convolution fusion | flops 536870912 | bytes 7340032 | tf_op jit(solution)/shard_map/while/body/eval_jaxpr/hps,shd->phd/dot_general | solution.py:138
  130.3 26.0 %collective-permute-done.2 = f32[8,128,128]{2,1,0:T(8,128)S(1)} collective-permute-done((f32[8,128,128]{2,1,0:T(8,128)S(1)}, f32[8,128,128]{2,1,0:T(8,128)S(1)}, u32[]{:S(2)}, u32[]{:S(2)}) %collective-permute-start.2) | collective-permute-done | bytes 524320 | tf_op jit(solution)/shard_map/ppermute | solution.py:30
  157.1 2.3 fusion
  159.4 2.9 %copy.116 = f32[512,8,128]{2,0,1:T(8,128)} copy(f32[512,8,128]{0,2,1:T(8,128)} %fusion) | data formatting | bytes 4194304 | tf_op jit(solution)/shard_map/reduce_sum | solution.py:160
  162.3 2.4 fusion.6
  164.7 1.6 copy.117
  166.4 2.3 convert_element_type.561
  168.7 4.5 %all-to-all-start.4 = ((bf16[4,128,1024]{2,1,0:T(8,128)(2,1)}), bf16[4,128,1024]{2,1,0:T(8,128)(2,1)}, u32[]{:S(2)}, u32[]{:S(2)}) async-start(bf16[4,128,1024]{2,1,0:T(8,128)(2,1)} %convert_element_type.561), calls=%async_computation.4 | async-start | bytes 2097152 | tf_op jit(solution)/shard_map/all_to_all | solution.py:188
  173.1 3.9 %fusion.1 = f32[512,8,128]{0,2,1:T(8,128)} fusion(f32[3,512,8]{1,0,2:T(4,128)S(1)} %copy.99, bf16[512,8,128,1]{2,1,0,3:T(8,128)(2,1)} %bitcast.134, bf16[1,8,128,128]{3,2,1,0:T(8,128)(2,1)} %copy-done.10, bf16[1,8,128,128]{3,2,1,0:T(8,128)(2,1)} %copy-done.9, bf16[1,8,128,128]{3,2,1,0:T(8,128)(2,1)S(1)} %copy-done.8), kind=kOutput, calls=%fused_computation.6 | convolution fusion | flops 406061056 | bytes 3981312 | tf_op jit(solution)/shard_map/phd,bhde->bphe/dot_general | solution.py:157
  177.0 2.9 %copy.104 = f32[512,8,128]{2,0,1:T(8,128)} copy(f32[512,8,128]{0,2,1:T(8,128)} %fusion.1) | data formatting | bytes 4194304 | tf_op jit(solution)/shard_map/reduce_sum | solution.py:155
  179.9 4.1 %fusion.7 = bf16[512,8,128]{2,0,1:T(8,128)(2,1)S(1)} fusion(f32[512,8,128]{2,0,1:T(8,128)} %copy.104, bf16[8,512,512]{2,1,0:T(8,128)(2,1)} %multiply_convert_fusion.1, bf16[512,8,128]{2,1,0:T(8,128)(2,1)S(1)} %bitcast.127), kind=kOutput, calls=%fused_computation.16 | convolution fusion | flops 537919488 | bytes 8388608 | tf_op jit(solution)/shard_map/while/body/eval_jaxpr/hps,she->phe/dot_general | solution.py:131
  184.0 1.6 copy.105
  185.7 2.3 convert_element_type.558
  188.0 4.3 %all-to-all-start.3 = ((bf16[4,128,1024]{2,1,0:T(8,128)(2,1)}), bf16[4,128,1024]{2,1,0:T(8,128)(2,1)}, u32[]{:S(2)}, u32[]{:S(2)}) async-start(bf16[4,128,1024]{2,1,0:T(8,128)(2,1)} %convert_element_type.558), calls=%async_computation.3 | async-start | bytes 2097152 | tf_op jit(solution)/shard_map/all_to_all | solution.py:187
  194.6 1.8 fusion.9
  198.9 7.8 %all-to-all-done.3 = bf16[4,128,1024]{2,1,0:T(8,128)(2,1)} async-done(((bf16[4,128,1024]{2,1,0:T(8,128)(2,1)}), bf16[4,128,1024]{2,1,0:T(8,128)(2,1)}, u32[]{:S(2)}, u32[]{:S(2)}) %all-to-all-start.3) | async-done | bytes 1048608 | tf_op jit(solution)/shard_map/all_to_all | solution.py:187
  206.8 3.5 %all-to-all-start.6 = ((bf16[4,128,1024]{1,2,0:T(8,128)(2,1)}), bf16[4,128,1024]{1,2,0:T(8,128)(2,1)S(1)}, u32[]{:S(2)}, u32[]{:S(2)}) async-start(bf16[4,128,1024]{1,2,0:T(8,128)(2,1)} %copy.130), calls=%async_computation.7 | async-start | bytes 2097152 | tf_op jit(solution)/shard_map/all_to_all | solution.py:190
  210.3 3.6 %fusion.12 = f32[8,512,128]{2,1,0:T(8,128)S(1)} fusion(bf16[8,512,512]{2,1,0:T(8,128)(2,1)} %copy-done, bf16[512,8,128]{2,1,0:T(8,128)(2,1)S(1)} %bitcast.136), kind=kOutput, calls=%fused_computation.28 | convolution fusion | flops 536870912 | bytes 7340032 | tf_op jit(solution)/shard_map/while/body/eval_jaxpr/hps,phd->shd/dot_general | solution.py:141
  216.3 8.3 %all-to-all-done.6 = bf16[4,128,1024]{1,2,0:T(8,128)(2,1)S(1)} async-done(((bf16[4,128,1024]{1,2,0:T(8,128)(2,1)}), bf16[4,128,1024]{1,2,0:T(8,128)(2,1)S(1)}, u32[]{:S(2)}, u32[]{:S(2)}) %all-to-all-start.6) | async-done | bytes 1048608 | tf_op jit(solution)/shard_map/all_to_all | solution.py:190
  224.7 3.5 %all-to-all-start.5 = ((bf16[4,128,1024]{2,1,0:T(8,128)(2,1)}), bf16[4,128,1024]{2,1,0:T(8,128)(2,1)S(1)}, u32[]{:S(2)}, u32[]{:S(2)}) async-start(bf16[4,128,1024]{2,1,0:T(8,128)(2,1)} %all_to_all.103), calls=%async_computation.6 | async-start | bytes 2097152 | tf_op jit(solution)/shard_map/all_to_all | solution.py:189
  228.2 1.6 copy.118
  231.1 1.6 copy.106
  235.4 7.2 %all-to-all-done.5 = bf16[4,128,1024]{2,1,0:T(8,128)(2,1)S(1)} async-done(((bf16[4,128,1024]{2,1,0:T(8,128)(2,1)}), bf16[4,128,1024]{2,1,0:T(8,128)(2,1)S(1)}, u32[]{:S(2)}, u32[]{:S(2)}) %all-to-all-start.5) | async-done | bytes 1048608 | tf_op jit(solution)/shard_map/all_to_all | solution.py:189
  (89 shorter events, 24.7 us)
Async XLA Ops:
  7.2 11.2 %copy-start.11 = (s32[8,13,512]{2,0,1:T(8,128)S(1)}, s32[8,13,512]{2,0,1:T(8,128)}, u32[]{:S(2)}) copy-start(s32[8,13,512]{2,0,1:T(8,128)} %param.9) | copy-start | bytes 638980
  9.4 13.2 %collective-permute-start.3 = (bf16[128,1024]{1,0:T(8,128)(2,1)}, bf16[128,1024]{1,0:T(8,128)(2,1)}, u32[]{:S(2)}, u32[]{:S(2)}) collective-permute-start(bf16[128,1024]{1,0:T(8,128)(2,1)} %get-tuple-element.46), channel_id=1, source_target_pairs={{0,1},{1,0},{2,3},{3,2},{4,5},{5,4},{6,7},{7,6},{8,9},{9,8},{10,11... | collective-permute-start | bytes 786440 | tf_op jit(solution)/shard_map/ppermute | solution.py:18
  9.9 13.9 %collective-permute-start.4 = (bf16[128,1024]{1,0:T(8,128)(2,1)}, bf16[128,1024]{1,0:T(8,128)(2,1)}, u32[]{:S(2)}, u32[]{:S(2)}) collective-permute-start(bf16[128,1024]{1,0:T(8,128)(2,1)} %get-tuple-element.48), channel_id=1, source_target_pairs={{0,2},{1,3},{2,0},{3,1},{4,6},{5,7},{6,4},{7,5},{8,10},{9,11},{10,... | collective-permute-start | bytes 786440 | tf_op jit(solution)/shard_map/ppermute | solution.py:18
  12.4 12.6 %collective-permute-start.5 = (bf16[128,1024]{1,0:T(8,128)(2,1)}, bf16[128,1024]{1,0:T(8,128)(2,1)S(1)}, u32[]{:S(2)}, u32[]{:S(2)}) collective-permute-start(bf16[128,1024]{1,0:T(8,128)(2,1)} %get-tuple-element.45), channel_id=1, source_target_pairs={{0,3},{1,2},{2,1},{3,0},{4,7},{5,6},{6,5},{7,4},{8,11},{9,10},{10,... | collective-permute-start | bytes 786440 | tf_op jit(solution)/shard_map/ppermute | solution.py:18
  14.8 21.6 %all-to-all-start = ((bf16[128,4,1024]{2,0,1:T(8,128)(2,1)}), bf16[128,4,1024]{2,0,1:T(8,128)(2,1)S(1)}, u32[]{:S(2)}, u32[]{:S(2)}) async-start(bf16[128,4,1024]{2,0,1:T(8,128)(2,1)} %bitcast.119), calls=%async_computation | async-start | bytes 2097152 | tf_op jit(solution)/shard_map/all_to_all | solution.py:49
  36.4 20.7 %all-to-all-start.1 = ((bf16[128,4,1024]{2,0,1:T(8,128)(2,1)}), bf16[128,4,1024]{2,0,1:T(8,128)(2,1)}, u32[]{:S(2)}, u32[]{:S(2)}) async-start(bf16[128,4,1024]{2,0,1:T(8,128)(2,1)} %bitcast.118), calls=%async_computation.1 | async-start | bytes 2097152 | tf_op jit(solution)/shard_map/all_to_all | solution.py:50
  40.7 151.6 %reduce-scatter.2.cloned.1.call-start = ((), (), s32[]{:S(2)}) async-start(), calls=%async_computation.8 | async-start | bytes 4718592 | tf_op jit(solution)/shard_map/reduce_scatter | solution.py:99
  41.0 1.0 copy-start.2
  42.0 5.7 %copy-start.20 = (f32[8,1]{0,1:T(1,128)S(1)}, f32[8,1]{0,1:T(1,128)}, u32[]{:S(2)}) copy-start(f32[8,1]{0,1:T(1,128)} %and_select_fusion.3) | copy-start | bytes 100
  54.9 1.2 copy-start.6
  57.2 18.0 %all-to-all-start.2 = ((bf16[128,4,1024]{2,0,1:T(8,128)(2,1)}), bf16[128,4,1024]{2,0,1:T(8,128)(2,1)S(1)}, u32[]{:S(2)}, u32[]{:S(2)}) async-start(bf16[128,4,1024]{2,0,1:T(8,128)(2,1)} %bitcast.117), calls=%async_computation.2 | async-start | bytes 2097152 | tf_op jit(solution)/shard_map/all_to_all | solution.py:51
  75.2 1.0 copy-start.5
  77.7 22.1 %copy-start.3 = (bf16[64,8,8,128]{3,2,1,0:T(8,128)(2,1)S(1)}, bf16[64,8,8,128]{3,2,1,0:T(8,128)(2,1)}, u32[]{:S(2)}) copy-start(bf16[64,8,8,128]{3,2,1,0:T(8,128)(2,1)} %copy-done.2) | copy-start | bytes 3145732
  77.7 22.1 %copy-start.12 = (f32[8,512]{1,0:T(8,128)S(1)}, f32[8,512]{1,0:T(8,128)}, u32[]{:S(2)}) copy-start(f32[8,512]{1,0:T(8,128)} %get-tuple-element.58) | copy-start | bytes 49156
  77.7 22.1 %copy-start.13 = (f32[8,512]{1,0:T(8,128)S(1)}, f32[8,512]{1,0:T(8,128)}, u32[]{:S(2)}) copy-start(f32[8,512]{1,0:T(8,128)} %get-tuple-element.59) | copy-start | bytes 49156
  77.7 22.1 %copy-start.14 = (f32[8,512]{1,0:T(8,128)S(1)}, f32[8,512]{1,0:T(8,128)}, u32[]{:S(2)}) copy-start(f32[8,512]{1,0:T(8,128)} %get-tuple-element.60) | copy-start | bytes 49156
  77.7 22.1 %copy-start.15 = (f32[8,512]{1,0:T(8,128)S(1)}, f32[8,512]{1,0:T(8,128)}, u32[]{:S(2)}) copy-start(f32[8,512]{1,0:T(8,128)} %get-tuple-element.61) | copy-start | bytes 49156
  77.7 22.1 %copy-start.16 = (f32[8,512]{1,0:T(8,128)S(1)}, f32[8,512]{1,0:T(8,128)}, u32[]{:S(2)}) copy-start(f32[8,512]{1,0:T(8,128)} %get-tuple-element.62) | copy-start | bytes 49156
  77.7 22.1 %copy-start.17 = (f32[8,512]{1,0:T(8,128)S(1)}, f32[8,512]{1,0:T(8,128)}, u32[]{:S(2)}) copy-start(f32[8,512]{1,0:T(8,128)} %get-tuple-element.63) | copy-start | bytes 49156
  77.7 22.1 %copy-start.18 = (f32[8,512]{1,0:T(8,128)S(1)}, f32[8,512]{1,0:T(8,128)}, u32[]{:S(2)}) copy-start(f32[8,512]{1,0:T(8,128)} %get-tuple-element.64) | copy-start | bytes 49156
  77.8 22.1 %copy-start.19 = (f32[8,512]{1,0:T(8,128)S(1)}, f32[8,512]{1,0:T(8,128)}, u32[]{:S(2)}) copy-start(f32[8,512]{1,0:T(8,128)} %get-tuple-element.65) | copy-start | bytes 49156
  78.4 19.2 %collective-permute-start = (f32[8,128,128]{2,1,0:T(8,128)S(1)}, f32[8,128,128]{2,1,0:T(8,128)S(1)}, u32[]{:S(2)}, u32[]{:S(2)}) collective-permute-start(f32[8,128,128]{2,1,0:T(8,128)S(1)} %fusion.19), channel_id=1, source_target_pairs={{0,4},{4,0},{8,12},{12,8},{16,20},{20,16},{24,28},{28,24},{1,5},{5... | collective-permute-start | bytes 1572872 | tf_op jit(solution)/shard_map/ppermute | solution.py:30
  97.6 58.7 %copy-start.7 = (bf16[1,8,128,128]{3,2,1,0:T(8,128)(2,1)}, bf16[1,8,128,128]{3,2,1,0:T(8,128)(2,1)S(1)}, u32[]{:S(2)}) copy-start(bf16[1,8,128,128]{3,2,1,0:T(8,128)(2,1)S(1)} %get-tuple-element.49) | copy-start | bytes 786436
  97.7 16.3 %collective-permute-start.1 = (f32[8,128,128]{2,1,0:T(8,128)S(1)}, f32[8,128,128]{2,1,0:T(8,128)S(1)}, u32[]{:S(2)}, u32[]{:S(2)}) collective-permute-start(f32[8,128,128]{2,1,0:T(8,128)S(1)} %get-tuple-element.50), channel_id=1, source_target_pairs={{0,8},{8,0},{4,12},{12,4},{16,24},{24,16},{20,28},{28,20},{1,9},{9... | collective-permute-start | bytes 1572872 | tf_op jit(solution)/shard_map/ppermute | solution.py:30
  114.0 42.3 %copy-start.9 = (bf16[1,8,128,128]{3,2,1,0:T(8,128)(2,1)}, bf16[1,8,128,128]{3,2,1,0:T(8,128)(2,1)S(1)}, u32[]{:S(2)}) copy-start(bf16[1,8,128,128]{3,2,1,0:T(8,128)(2,1)S(1)} %get-tuple-element.51) | copy-start | bytes 786436
  114.0 42.3 %collective-permute-start.2 = (f32[8,128,128]{2,1,0:T(8,128)S(1)}, f32[8,128,128]{2,1,0:T(8,128)S(1)}, u32[]{:S(2)}, u32[]{:S(2)}) collective-permute-start(f32[8,128,128]{2,1,0:T(8,128)S(1)} %get-tuple-element.52), channel_id=1, source_target_pairs={{0,16},{16,0},{4,20},{20,4},{8,24},{24,8},{12,28},{28,12},{1,17},{... | collective-permute-start | bytes 1572872 | tf_op jit(solution)/shard_map/ppermute | solution.py:30
  125.7 2.0 copy-start
  156.4 0.7 copy-start.10
  164.7 8.4 %copy-start.8 = (bf16[1,8,128,128]{3,2,1,0:T(8,128)(2,1)S(1)}, bf16[1,8,128,128]{3,2,1,0:T(8,128)(2,1)}, u32[]{:S(2)}) copy-start(bf16[1,8,128,128]{3,2,1,0:T(8,128)(2,1)} %copy-done.7) | copy-start | bytes 786436
  168.7 19.3 %all-to-all-start.4 = ((bf16[4,128,1024]{2,1,0:T(8,128)(2,1)}), bf16[4,128,1024]{2,1,0:T(8,128)(2,1)}, u32[]{:S(2)}, u32[]{:S(2)}) async-start(bf16[4,128,1024]{2,1,0:T(8,128)(2,1)} %convert_element_type.561), calls=%async_computation.4 | async-start | bytes 2097152 | tf_op jit(solution)/shard_map/all_to_all | solution.py:188
  188.0 18.8 %all-to-all-start.3 = ((bf16[4,128,1024]{2,1,0:T(8,128)(2,1)}), bf16[4,128,1024]{2,1,0:T(8,128)(2,1)}, u32[]{:S(2)}, u32[]{:S(2)}) async-start(bf16[4,128,1024]{2,1,0:T(8,128)(2,1)} %convert_element_type.558), calls=%async_computation.3 | async-start | bytes 2097152 | tf_op jit(solution)/shard_map/all_to_all | solution.py:187
  192.3 2.3 copy-start.1
  196.4 13.9 %copy-start.4 = (bf16[64,8,8,128]{3,2,1,0:T(8,128)(2,1)S(1)}, bf16[64,8,8,128]{3,2,1,0:T(8,128)(2,1)}, u32[]{:S(2)}) copy-start(bf16[64,8,8,128]{3,2,1,0:T(8,128)(2,1)} %copy-done.2) | copy-start | bytes 3145732
  206.8 17.9 %all-to-all-start.6 = ((bf16[4,128,1024]{1,2,0:T(8,128)(2,1)}), bf16[4,128,1024]{1,2,0:T(8,128)(2,1)S(1)}, u32[]{:S(2)}, u32[]{:S(2)}) async-start(bf16[4,128,1024]{1,2,0:T(8,128)(2,1)} %copy.130), calls=%async_computation.7 | async-start | bytes 2097152 | tf_op jit(solution)/shard_map/all_to_all | solution.py:190
  224.7 17.9 %all-to-all-start.5 = ((bf16[4,128,1024]{2,1,0:T(8,128)(2,1)}), bf16[4,128,1024]{2,1,0:T(8,128)(2,1)S(1)}, u32[]{:S(2)}, u32[]{:S(2)}) async-start(bf16[4,128,1024]{2,1,0:T(8,128)(2,1)} %all_to_all.103), calls=%async_computation.6 | async-start | bytes 2097152 | tf_op jit(solution)/shard_map/all_to_all | solution.py:189
Sparse Core Ops, SparseCore 0:
  55.0 102.2 reduce-scatter.1
